TPU v7x, 32 devices: a whole 2x2x4 slice. The times are simulated.
32 devices in a mesh: dp: 4 (over z), seq: 2 (over x), tensor: 4 (over y, core).
Axes of the slice: x: 2, y: 2, z: 4, core: 2. Of those that a mesh axis runs over, the one named last changes fastest.
Arguments:
- hidden_in: bfloat16 [16384, 2880], P(('dp', 'seq', 'tensor')), parts along dimension 0, may hold values from -6 to 6
- norm_gain: float32 [2880], replicated, may hold values from 0.5 to 1.5
- conv_weight: float32 [4, 2880], replicated, may hold values from -3 to 3
- w_query: bfloat16 [2880, 2048], P(None, 'tensor'), may hold values from -32 to 32
- w_key: bfloat16 [2880, 512], P(None, 'tensor'), may hold values from -1 to 1
- w_value: bfloat16 [2880, 512], P(None, 'tensor'), may hold values from -0.109375 to 0.109375
- w_out: bfloat16 [2048, 2880], P('tensor'), may hold values from -0.125 to 0.125
- doc_ids: int32 [16384], P(('dp', 'seq')), parts along dimension 0, may hold values from 0 to 15, never falling along the last dimension, each value on 1 to 1024 neighbouring positions
Outputs:
- hidden_out: bfloat16 [16384, 2880], P(('dp', 'seq', 'tensor')), parts along dimension 0
There are 4 independent parts, one for each index of `dp`. A program takes and returns all parts, laid end to end along the dimension named above; an argument that names none is the same for every part. Nothing has to cross between parts.
Inputs may be any that keep to these rules, and one draw needn't show every extreme that they name: `doc_ids`: document numbers never fall along a window's tokens.
All inputs are finite; a program needn't handle non-finite values.
Results may differ from a plain program's by a relative error of at most 0.011.
Values may be sent and summed in bfloat16 or wider, within the bound.
A program may use at most 128 MiB of HBM per device.

v0:
```python
import math

import jax
import jax.numpy as jnp
from jax import lax
from jax.sharding import PartitionSpec as P

HEAD = 64
WINDOW = 128
QBLOCK = 512


eps = 1e-05
rope_base = 150000.0


def passed_along(array, axis, by):
    devices = lax.axis_size(axis)
    pairs = [(i, i + by) for i in range(devices) if 0 <= i + by < devices]
    return lax.ppermute(array, axis, pairs)


def rotate(values, positions):
    rows = values.shape[0]
    half = HEAD // 2
    frequency = jnp.exp(jnp.arange(half, dtype=jnp.float32) * (-2.0 * math.log(rope_base) / HEAD))
    angle = positions.astype(jnp.float32)[:, None] * frequency[None, :]
    cosine = jnp.cos(angle)[:, None, :]
    sine = jnp.sin(angle)[:, None, :]
    shaped = values.reshape(rows, -1, HEAD)
    first = shaped[:, :, :half]
    second = shaped[:, :, half:]
    turned = jnp.concatenate(
        [first * cosine - second * sine, second * cosine + first * sine], axis=2
    )
    return turned.reshape(rows, -1)


def attend(queries, keys, values, query_pos, key_pos, query_doc, key_doc):
    scores = jnp.einsum("qhgd,khd->hgqk", queries, keys, preferred_element_type=jnp.float32) * (
        1.0 / math.sqrt(HEAD)
    )
    visible = (key_pos[None, :] <= query_pos[:, None]) & (
        key_pos[None, :] > query_pos[:, None] - WINDOW
    )
    visible = visible & (key_pos[None, :] >= 0) & (key_doc[None, :] == query_doc[:, None])
    scores = jnp.where(visible[None, None, :, :], scores, -jnp.inf)
    largest = jnp.max(scores, axis=3, keepdims=True)
    weights = jnp.exp(scores - largest)
    total = jnp.sum(weights, axis=3)
    rounded = weights.astype(jnp.bfloat16)
    summed = jnp.einsum("hgqk,khd->qhgd", rounded, values, preferred_element_type=jnp.float32)
    result = summed / jnp.transpose(total, (2, 0, 1))[:, :, :, None]
    return result.reshape(result.shape[0], -1).astype(jnp.bfloat16)


def local(hidden_in, norm_gain, conv_weight, w_query, w_key, w_value, w_out, doc_ids):
    rows = hidden_in.shape[0]
    width = hidden_in.shape[1]
    taps = conv_weight.shape[0]
    inputs = hidden_in.astype(jnp.float32)
    mean_square = jnp.mean(inputs * inputs, axis=1, keepdims=True)
    normed = (inputs * lax.rsqrt(mean_square + eps) * norm_gain[None, :]).astype(jnp.bfloat16)
    earlier = passed_along(normed[rows - (taps - 1) :], ("seq", "tensor"), 1)
    extended = jnp.concatenate([earlier, normed], axis=0).astype(jnp.float32)
    convolved = jnp.zeros((rows, width), jnp.float32)
    for tap in range(taps):
        convolved = (
            convolved + conv_weight[tap][None, :] * extended[taps - 1 - tap : taps - 1 - tap + rows]
        )
    mixed = convolved.astype(jnp.bfloat16)
    query_cols = w_query.shape[1]
    key_cols = w_key.shape[1]
    piece = lax.all_gather(mixed, "tensor", axis=0, tiled=True)
    projected = jnp.concatenate(
        [
            jnp.dot(piece, w_query, preferred_element_type=jnp.float32),
            jnp.dot(piece, w_key, preferred_element_type=jnp.float32),
            jnp.dot(piece, w_value, preferred_element_type=jnp.float32),
        ],
        axis=1,
    )
    span = projected.shape[0]
    offset = lax.axis_index("seq") * span
    positions = offset + jnp.arange(span, dtype=jnp.int32)
    queries = rotate(projected[:, :query_cols], positions).astype(jnp.bfloat16)
    keys = rotate(projected[:, query_cols : query_cols + key_cols], positions).astype(jnp.bfloat16)
    values = projected[:, query_cols + key_cols :].astype(jnp.bfloat16)
    key_rim, value_rim = passed_along((keys[span - WINDOW :], values[span - WINDOW :]), "seq", 1)
    doc_rim = passed_along(doc_ids[span - WINDOW :], "seq", 1)
    heads_here = query_cols // HEAD
    kv_here = key_cols // HEAD
    groups = heads_here // kv_here
    query_four = queries.reshape(span, kv_here, groups, HEAD)
    key_ext = jnp.concatenate([key_rim, keys], axis=0).reshape(span + WINDOW, kv_here, HEAD)
    value_ext = jnp.concatenate([value_rim, values], axis=0).reshape(span + WINDOW, kv_here, HEAD)
    doc_ext = jnp.concatenate([doc_rim, doc_ids], axis=0)
    pos_ext = offset - WINDOW + jnp.arange(span + WINDOW, dtype=jnp.int32)

    def one_block(index):
        begin = index * QBLOCK
        block_q = lax.dynamic_slice_in_dim(query_four, begin, QBLOCK, 0)
        block_k = lax.dynamic_slice_in_dim(key_ext, begin, QBLOCK + WINDOW, 0)
        block_v = lax.dynamic_slice_in_dim(value_ext, begin, QBLOCK + WINDOW, 0)
        query_pos = lax.dynamic_slice_in_dim(positions, begin, QBLOCK, 0)
        key_pos = lax.dynamic_slice_in_dim(pos_ext, begin, QBLOCK + WINDOW, 0)
        query_doc = lax.dynamic_slice_in_dim(doc_ids, begin, QBLOCK, 0)
        key_doc = lax.dynamic_slice_in_dim(doc_ext, begin, QBLOCK + WINDOW, 0)
        return attend(block_q, block_k, block_v, query_pos, key_pos, query_doc, key_doc)

    blocks = lax.map(one_block, jnp.arange(span // QBLOCK, dtype=jnp.int32))
    attended = blocks.reshape(span, query_cols)
    regrouped = lax.all_to_all(attended, "tensor", split_axis=0, concat_axis=1, tiled=True)
    summed = jnp.dot(
        regrouped,
        lax.all_gather(w_out, "tensor", axis=0, tiled=True),
        preferred_element_type=jnp.float32,
    )
    return (inputs + summed).astype(jnp.bfloat16)


def solution(mesh):
    in_specs = (
        P(("dp", "seq", "tensor"), None),
        P(),
        P(),
        P(None, "tensor"),
        P(None, "tensor"),
        P(None, "tensor"),
        P("tensor", None),
        P(("dp", "seq")),
    )
    out_specs = P(("dp", "seq", "tensor"), None)
    return jax.shard_map(local, mesh=mesh, in_specs=in_specs, out_specs=out_specs, check_vma=False)
```

profile of v0, /device:TPU:27, one launch (start us, length us, event | category | flops | bytes accessed | tf_op | source)
XLA Modules:
  0.0 233.0 jit_solution(2197101722472031939)
XLA Ops:
  6.5 2.7 %fusion.21 = f32[512]{0:T(512)S(1)} fusion(bf16[512,2880]{0,1:T(8,128)(2,1)} %param.10), kind=kLoop, calls=%fused_computation.26 | loop fusion | flops 4423168 | bytes 2951168 | tf_op jit(solution)/shard_map/reduce_sum | solution.py:62
  9.2 2.5 %fusion.23 = bf16[512,2880]{0,1:T(8,128)(2,1)S(1)} fusion(bf16[512,2880]{0,1:T(8,128)(2,1)} %param.10, f32[2880]{0:T(1024)} %param.11, f32[512]{0:T(512)S(1)} %add_rsqrt_fusion), kind=kLoop, calls=%fused_computation.28 | loop fusion | flops 5898240 | bytes 5911808 | tf_op jit(solution)/shard_map/convert_element_type | solution.py:63
  15.9 3.7 %collective-permute-start = (bf16[3,2880]{1,0:T(4,128)(2,1)S(1)}, bf16[3,2880]{1,0:T(4,128)(2,1)S(1)}, u32[]{:S(2)}, u32[]{:S(2)}) collective-permute-start(bf16[3,2880]{1,0:T(4,128)(2,1)S(1)} %copy.14), channel_id=1, source_target_pairs={{0,1},{1,2},{2,3},{3,4},{4,5},{5,6},{6,7},{8,9},{9,10},{10,11},{11... | collective-permute-start | bytes 51848 | tf_op jit(solution)/shard_map/ppermute | solution.py:20
  21.7 3.7 %maximum_convert_fusion = f32[515,2880]{0,1:T(8,128)S(1)} fusion(bf16[512,2880]{0,1:T(8,128)(2,1)} %copy-done.2, bf16[3,2880]{0,1:T(8,128)(2,1)} %copy.15), kind=kLoop, calls=%fused_computation.38 | loop fusion | flops 5932800 | bytes 8899200 | tf_op jit(solution)/shard_map/convert_element_type | solution.py:65
  25.4 8.3 %fusion.26 = bf16[512,2880]{0,1:T(8,128)(2,1)} fusion(f32[515,2880]{0,1:T(8,128)S(1)} %maximum_convert_fusion, f32[2880]{0:T(1024)S(1)} %get-tuple-element.143, f32[2880]{0:T(1024)S(1)} %get-tuple-element.144, f32[2880]{0:T(1024)S(1)} %get-tuple-element.142, f32[2880]{0:T(1024)S(1)} %get-tuple-element.141), kind=kLoop, calls=%fused_computation.32 | loop fusion | flops 11796480 | bytes 26588160 | tf_op jit(solution)/shard_map/convert_element_type | solution.py:71
  36.2 1.9 collective-permute-done.2
  38.1 75.3 %all-gather.3.cloned.1.call-done = bf16[2048,2880]{0,1:T(8,128)(2,1)} async-done(((bf16[512,2880]{0,1:T(8,128)(2,1)}), bf16[2048,2880]{0,1:T(8,128)(2,1)}) %all-gather.3.cloned.1.call-update) | async-done | bytes 11796496 | tf_op jit(solution)/shard_map/all_gather | solution.py:74
  113.4 6.5 %fusion.31 = f32[2048,128]{0,1:T(8,128)S(1)} fusion(bf16[2048,2880]{0,1:T(8,128)(2,1)} %all-gather.3.cloned.1.call-done, bf16[2880,128]{1,0:T(8,128)(2,1)} %param.14), kind=kOutput, calls=%fused_computation.63 | convolution fusion | flops 1509949440 | bytes 13582336 | tf_op jit(solution)/shard_map/dot_general | solution.py:78
  122.3 3.5 %convolution_convert_fusion = bf16[2048,128]{1,0:T(8,128)(2,1)S(1)} fusion(bf16[2048,2880]{0,1:T(8,128)(2,1)S(1)} %copy-done.5, bf16[2880,128]{1,0:T(8,128)(2,1)S(1)} %copy-done.6), kind=kOutput, calls=%fused_computation.39 | convolution fusion | flops 1510211584 | bytes 13058048 | tf_op jit(solution)/shard_map/dot_general | solution.py:79
  127.1 7.2 %fusion.32 = f32[2048,512]{0,1:T(8,128)S(1)} fusion(bf16[2048,2880]{0,1:T(8,128)(2,1)S(1)} %copy-done.5, bf16[2880,512]{1,0:T(8,128)(2,1)S(1)} %copy-done), kind=kOutput, calls=%fused_computation.64 | convolution fusion | flops 6039797760 | bytes 18939904 | tf_op jit(solution)/shard_map/dot_general | solution.py:77
  136.4 42.9 %while.12 = (s32[]{:T(128)}, bf16[4,512,512]{1,2,0:T(8,128)(2,1)}, s32[4]{0:T(128)S(1)}, bf16[2176,2,64]{0,2,1:T(8,128)(2,1)}, s32[2176]{0:T(1024)S(1)}, /*index...) while((s32[]{:T(128)}, bf16[4,512,512]{1,2,0:T(8,128)(2,1)}, ...), condition=%wide.region_4.5_spmd, body=%wide.region_1.4_spmd.sunk | while | flops 702407808 | bytes 35308540 | solution.py:111
  140.5 2.2 fusion.48
  142.7 3.7 %divide_convert_fusion.2 = bf16[512,2,4,64]{0,3,2,1:T(8,128)(2,1)S(1)} fusion(f32[2,640,512,4]{2,1,3,0:T(8,128)S(1)} %get-tuple-element.248, f32[2,4,512]{2,1,0:T(4,128)S(1)} %get-tuple-element.249, pred[512,640]{0,1:T(8,128)(4,1)S(1)} %compare_and_fusion.2, f32[512,2,4]{0,2,1:T(4,128)S(1)} %bitcast.75, bf16[2176,2,64]{0,2,1:T(8,128)(2,1)} %get-tuple-element.283, ...), kind=kOutput, calls=%fused_computation.9.clone.1 | convolution fusion | flops 346554368 | bytes 11534340 | tf_op jit(solution)/shard_map/while/body/eval_jaxpr/hgqk,khd->qhgd/dot_general | solution.py:52
  149.4 1.8 fusion.47
  151.2 2.2 fusion.48
  153.3 3.7 %divide_convert_fusion.2 = bf16[512,2,4,64]{0,3,2,1:T(8,128)(2,1)S(1)} fusion(f32[2,640,512,4]{2,1,3,0:T(8,128)S(1)} %get-tuple-element.248, f32[2,4,512]{2,1,0:T(4,128)S(1)} %get-tuple-element.249, pred[512,640]{0,1:T(8,128)(4,1)S(1)} %compare_and_fusion.2, f32[512,2,4]{0,2,1:T(4,128)S(1)} %bitcast.75, bf16[2176,2,64]{0,2,1:T(8,128)(2,1)} %get-tuple-element.283, ...), kind=kOutput, calls=%fused_computation.9.clone.1 | convolution fusion | flops 346554368 | bytes 11534340 | tf_op jit(solution)/shard_map/while/body/eval_jaxpr/hgqk,khd->qhgd/dot_general | solution.py:52
  161.8 2.2 fusion.48
  164.0 3.7 %divide_convert_fusion.2 = bf16[512,2,4,64]{0,3,2,1:T(8,128)(2,1)S(1)} fusion(f32[2,640,512,4]{2,1,3,0:T(8,128)S(1)} %get-tuple-element.248, f32[2,4,512]{2,1,0:T(4,128)S(1)} %get-tuple-element.249, pred[512,640]{0,1:T(8,128)(4,1)S(1)} %compare_and_fusion.2, f32[512,2,4]{0,2,1:T(4,128)S(1)} %bitcast.75, bf16[2176,2,64]{0,2,1:T(8,128)(2,1)} %get-tuple-element.283, ...), kind=kOutput, calls=%fused_computation.9.clone.1 | convolution fusion | flops 346554368 | bytes 11534340 | tf_op jit(solution)/shard_map/while/body/eval_jaxpr/hgqk,khd->qhgd/dot_general | solution.py:52
  172.5 2.2 fusion.48
  174.6 3.7 %divide_convert_fusion.2 = bf16[512,2,4,64]{0,3,2,1:T(8,128)(2,1)S(1)} fusion(f32[2,640,512,4]{2,1,3,0:T(8,128)S(1)} %get-tuple-element.248, f32[2,4,512]{2,1,0:T(4,128)S(1)} %get-tuple-element.249, pred[512,640]{0,1:T(8,128)(4,1)S(1)} %compare_and_fusion.2, f32[512,2,4]{0,2,1:T(4,128)S(1)} %bitcast.75, bf16[2176,2,64]{0,2,1:T(8,128)(2,1)} %get-tuple-element.283, ...), kind=kOutput, calls=%fused_computation.9.clone.1 | convolution fusion | flops 346554368 | bytes 11534340 | tf_op jit(solution)/shard_map/while/body/eval_jaxpr/hgqk,khd->qhgd/dot_general | solution.py:52
  179.3 4.6 %all-to-all-start = ((bf16[4,512,512]{1,2,0:T(8,128)(2,1)}), bf16[4,512,512]{1,2,0:T(8,128)(2,1)}, u32[]{:S(2)}, u32[]{:S(2)}) async-start(bf16[4,512,512]{1,2,0:T(8,128)(2,1)} %get-tuple-element.130), calls=%async_computation | async-start | bytes 4194304 | tf_op jit(solution)/shard_map/all_to_all | solution.py:113
  183.9 12.5 %all-gather.5.cloned.1.call-done = bf16[2048,2880]{0,1:T(8,128)(2,1)} async-done(((bf16[512,2880]{0,1:T(8,128)(2,1)}), bf16[2048,2880]{0,1:T(8,128)(2,1)}) %all-gather.5.cloned.1.call-update) | async-done | bytes 11796496 | tf_op jit(solution)/shard_map/all_gather | solution.py:116
  196.5 16.5 %all-to-all-done = bf16[4,512,512]{1,2,0:T(8,128)(2,1)} async-done(((bf16[4,512,512]{1,2,0:T(8,128)(2,1)}), bf16[4,512,512]{1,2,0:T(8,128)(2,1)}, u32[]{:S(2)}, u32[]{:S(2)}) %all-to-all-start) | async-done | bytes 2097184 | tf_op jit(solution)/shard_map/all_to_all | solution.py:113
  213.0 13.2 %fusion.24 = bf16[512,2880]{0,1:T(8,128)(2,1)} fusion(bf16[512,2880]{0,1:T(8,128)(2,1)} %param.10, bf16[2048,2880]{0,1:T(8,128)(2,1)} %all-gather.5.cloned.1.call-done, bf16[512,2048]{0,1:T(8,128)(2,1)} %bitcast.17), kind=kOutput, calls=%fused_computation.29 | convolution fusion | flops 6044221440 | bytes 19791872 | tf_op jit(solution)/shard_map/dot_general | solution.py:114
  (78 shorter events, 29.2 us)
Async XLA Ops:
  6.5 120.6 %copy-start = (bf16[2880,512]{1,0:T(8,128)(2,1)S(1)}, bf16[2880,512]{1,0:T(8,128)(2,1)}, u32[]{:S(2)}) copy-start(bf16[2880,512]{1,0:T(8,128)(2,1)} %param.13) | copy-start | bytes 8847364
  6.5 13.1 %copy-start.3 = (f32[4,2880]{1,0:T(4,128)S(1)}, f32[4,2880]{1,0:T(4,128)}, u32[]{:S(2)}) copy-start(f32[4,2880]{1,0:T(4,128)} %param.12) | copy-start | bytes 138244
  6.5 106.9 %all-gather.3.cloned.1.call-start = ((), (), s32[]{:S(2)}) async-start(), calls=%async_computation.1 | async-start | bytes 14745600 | tf_op jit(solution)/shard_map/all_gather | solution.py:74
  11.8 1.6 copy-start.2
  15.9 4.6 %collective-permute-start = (bf16[3,2880]{1,0:T(4,128)(2,1)S(1)}, bf16[3,2880]{1,0:T(4,128)(2,1)S(1)}, u32[]{:S(2)}, u32[]{:S(2)}) collective-permute-start(bf16[3,2880]{1,0:T(4,128)(2,1)S(1)} %copy.14), channel_id=1, source_target_pairs={{0,1},{1,2},{2,3},{3,4},{4,5},{5,6},{6,7},{8,9},{9,10},{10,11},{11... | collective-permute-start | bytes 51848 | tf_op jit(solution)/shard_map/ppermute | solution.py:20
  25.4 8.4 %copy-start.4 = (s32[2048]{0:T(1024)S(1)}, s32[2048]{0:T(1024)}, u32[]{:S(2)}) copy-start(s32[2048]{0:T(1024)} %param.17) | copy-start | bytes 24580
  33.7 162.7 %all-gather.5.cloned.1.call-start = ((), (), s32[]{:S(2)}) async-start(), calls=%async_computation.2 | async-start | bytes 14745600 | tf_op jit(solution)/shard_map/all_gather | solution.py:116
  33.8 4.3 %collective-permute-start.2 = (s32[128]{0:T(128)S(1)}, s32[128]{0:T(128)S(1)}, u32[]{:S(2)}, u32[]{:S(2)}) collective-permute-start(s32[128]{0:T(128)S(1)} %slice.61), channel_id=1, source_target_pairs={{0,4},{1,5},{2,6},{3,7},{8,12},{9,13},{10,14},{11,15},{16,20},{17,... | collective-permute-start | bytes 1544 | tf_op jit(solution)/shard_map/ppermute | solution.py:20
  113.4 8.9 %copy-start.5 = (bf16[2048,2880]{0,1:T(8,128)(2,1)S(1)}, bf16[2048,2880]{0,1:T(8,128)(2,1)}, u32[]{:S(2)}) copy-start(bf16[2048,2880]{0,1:T(8,128)(2,1)} %all-gather.3.cloned.1.call-done) | copy-start | bytes 35389444
  113.4 8.9 %copy-start.6 = (bf16[2880,128]{1,0:T(8,128)(2,1)S(1)}, bf16[2880,128]{1,0:T(8,128)(2,1)}, u32[]{:S(2)}) copy-start(bf16[2880,128]{1,0:T(8,128)(2,1)} %param.15) | copy-start | bytes 2211844
  120.6 15.7 %collective-permute-start.3 = (bf16[128,128]{0,1:T(8,128)(2,1)}, bf16[128,128]{0,1:T(8,128)(2,1)S(1)}, u32[]{:S(2)}, u32[]{:S(2)}) collective-permute-start(bf16[128,128]{0,1:T(8,128)(2,1)} %bitcast.11), channel_id=1, source_target_pairs={{0,4},{1,5},{2,6},{3,7},{8,12},{9,13},{10,14},{11,15},{16,20},{17,... | collective-permute-start | bytes 98312 | tf_op jit(solution)/shard_map/ppermute | solution.py:20
  125.8 9.4 %collective-permute-start.1 = (bf16[128,128]{1,0:T(8,128)(2,1)S(1)}, bf16[128,128]{1,0:T(8,128)(2,1)S(1)}, u32[]{:S(2)}, u32[]{:S(2)}) collective-permute-start(bf16[128,128]{1,0:T(8,128)(2,1)S(1)} %slice.73), channel_id=1, source_target_pairs={{0,4},{1,5},{2,6},{3,7},{8,12},{9,13},{10,14},{11,15},{16,20},{17,... | collective-permute-start | bytes 98312 | tf_op jit(solution)/shard_map/ppermute | solution.py:20
  179.3 33.7 %all-to-all-start = ((bf16[4,512,512]{1,2,0:T(8,128)(2,1)}), bf16[4,512,512]{1,2,0:T(8,128)(2,1)}, u32[]{:S(2)}, u32[]{:S(2)}) async-start(bf16[4,512,512]{1,2,0:T(8,128)(2,1)} %get-tuple-element.130), calls=%async_computation | async-start | bytes 4194304 | tf_op jit(solution)/shard_map/all_to_all | solution.py:113
  213.0 13.2 %copy-start.1 = (bf16[2880,512]{1,0:T(8,128)(2,1)S(1)}, bf16[2880,512]{1,0:T(8,128)(2,1)}, u32[]{:S(2)}) copy-start(bf16[2880,512]{1,0:T(8,128)(2,1)} %param.13) | copy-start | bytes 8847364
Sparse Core Ops, SparseCore 0:
  33.9 79.4 all-gather.2
  115.0 81.4 all-gather.4
where the time goes:
time: 235 us; the launch traced here: 233 us
  waiting for transfers between devices  107 us (46%)
  matrix products  52.4 us (22%)
  other arithmetic  31.9 us (14%)
  between operations  13.7 us (6%)
  local copies, waits for them, and re-layouts  12.9 us (5%)
  starting transfers between devices  12.6 us (5%)
  loops' own time  2.61 us (1%)
    all_gather x1, waiting for transfers between devices, local(): piece = lax.all_gather(mixed, 'tensor', axis=0, tiled=True)  75.3 us
    all_to_all x1, waiting for transfers between devices, local(): lax.all_to_all(attended, 'tensor', split_axis=0, concat_axis=1, tiled=True)  16.5 us
    dot_general x4, matrix products, attend(): jnp.einsum('hgqk,khd->qhgd', rounded, values, preferred_element_type=jnp....  14.9 us
    dot_general x1, matrix products, local(): jnp.dot(regrouped, lax.all_gather(w_out, 'tensor', axis=0, tiled=True), p...  13.2 us
    all_gather x1, waiting for transfers between devices, local(): lax.all_gather(w_out, 'tensor', axis=0, tiled=True)  12.5 us
    reduce_sum x4, other arithmetic, attend(): total = jnp.sum(weights, axis=3)  8.69 us
    convert_element_type x1, other arithmetic, local(): mixed = convolved.astype(jnp.bfloat16)  8.31 us
    ppermute x4, starting transfers between devices, passed_along(): return lax.ppermute(array, axis, pairs)  7.88 us
  transfers between devices with their start and end apart: 7, of which 5 were waited for; matrix products, arithmetic and copies ran while one was open for 26% of the time, Pallas kernels for 0%

commit v1 on v0

v1 whole, which is shorter than its diff:
```python
import math

import jax
import jax.numpy as jnp
from jax import lax
from jax.experimental import pallas as pl
from jax.experimental.pallas import tpu as pltpu
from jax.sharding import PartitionSpec as P

HEAD = 64
WINDOW = 128
HALO = 144
PAD = HALO - WINDOW
LANES = 128
eps = 1e-05
rope_base = 150000.0
BF = jnp.bfloat16
F32 = jnp.float32


def kernel(seq_size, tensor_size, hidden, gain, taps, wq, wk, wv, wout, doc_row, doc_col, cos, sin, out,
           ext, normed, mixed, wqkv, wo, q_s, k_s, v_s, att, acc, docs, bias,
           load_sem, y_s, y_r, x_s, x_r, z_s, z_r, n_s, n_r, d_s, d_r, h_s, h_r):
    rows, width = hidden.shape
    qc, kc = wq.shape[1], wk.shape[1]
    cols = qc + 2 * kc
    ntaps = taps.shape[0]
    full = rows + WINDOW
    dp, seq, tensor = lax.axis_index("dp"), lax.axis_index("seq"), lax.axis_index("tensor")

    def other(i, bit):
        return i + bit * (1 - 2 * ((i // bit) % 2))

    y_dev = (dp, seq, other(tensor, 2))
    n_dev = (dp, seq, other(tensor, 1))
    x_dev = (dp, other(seq, 1), tensor)
    z_dev = (other(dp, 1), seq, tensor)
    place = seq * tensor_size + tensor
    has_prev = place > 0
    has_next = place < seq_size * tensor_size - 1
    nxt, prv = place + 1, place - 1
    next_dev = (dp, nxt // tensor_size, nxt % tensor_size)
    prev_dev = (dp, prv // tensor_size, prv % tensor_size)
    MESH = pl.DeviceIdType.MESH

    barrier = pltpu.get_barrier_semaphore()
    for dev in (y_dev, n_dev, x_dev, z_dev):
        pl.semaphore_signal(barrier, inc=1, device_id=dev, device_id_type=MESH)

    @pl.when(has_prev)
    def _():
        pl.semaphore_signal(barrier, inc=1, device_id=prev_dev, device_id_type=MESH)

    @pl.when(has_next)
    def _():
        pl.semaphore_signal(barrier, inc=1, device_id=next_dev, device_id_type=MESH)

    load_w = [
        pltpu.make_async_copy(wq, wqkv.at[0, :, pl.ds(0, qc)], load_sem.at[0]),
        pltpu.make_async_copy(wk, wqkv.at[0, :, pl.ds(qc, kc)], load_sem.at[1]),
        pltpu.make_async_copy(wv, wqkv.at[0, :, pl.ds(qc + kc, kc)], load_sem.at[2]),
    ]
    load_o = pltpu.make_async_copy(wout, wo.at[0], load_sem.at[3])
    load_h = pltpu.make_async_copy(hidden, ext.at[pl.ds(HALO, rows)], load_sem.at[4])
    load_d = pltpu.make_async_copy(doc_row, docs.at[:, pl.ds(WINDOW, rows)], load_sem.at[5])
    for c in load_w:
        c.start()
    load_h.start()
    load_d.start()
    load_o.start()
    pl.semaphore_wait(barrier, 4 + jnp.where(has_prev, 1, 0) + jnp.where(has_next, 1, 0))

    halo_h = pltpu.make_async_remote_copy(
        src_ref=hidden.at[pl.ds(rows - HALO, HALO)], dst_ref=ext.at[pl.ds(0, HALO)],
        send_sem=h_s.at[0], recv_sem=h_r.at[0], device_id=next_dev, device_id_type=MESH)
    halo_d = pltpu.make_async_remote_copy(
        src_ref=doc_row.at[:, pl.ds(rows - WINDOW, WINDOW)], dst_ref=docs.at[:, pl.ds(0, WINDOW)],
        send_sem=h_s.at[1], recv_sem=h_r.at[1], device_id=next_dev, device_id_type=MESH)

    @pl.when(has_next)
    def _():
        halo_h.start()
        halo_d.start()

    wrow, orow = width // 4, qc // 4
    wpart = wrow // 3
    osize = (48, 48, 32) if orow == 128 else (orow // 2, orow // 4, orow // 4)
    ostart = (0, osize[0], osize[0] + osize[1])

    def part(buf, slot, q, j):
        if buf == 0:
            return wqkv.at[slot, pl.ds(pl.multiple_of(q * wrow + j * wpart, 16), wpart)]
        return wo.at[slot, pl.ds(pl.multiple_of(q * orow + ostart[j], 16), osize[j])]

    xb, zb = seq % 2, dp % 2
    quarter = (xb * 2 + zb, (1 - xb) * 2 + zb, xb * 2 + 1 - zb, (1 - xb) * 2 + 1 - zb)
    sent = []

    def copy(buf, role, j, src_slot, dst_slot, ss, rs, k, dev):
        return pltpu.make_async_remote_copy(
            src_ref=part(buf, src_slot, quarter[role], j), dst_ref=part(buf, dst_slot, quarter[role], j),
            send_sem=ss.at[buf, k], recv_sem=rs.at[buf, k], device_id=dev, device_id_type=MESH)

    def go(c):
        c.start()
        sent.append(c)

    def y_copy(buf, k):
        role, j = ((0, 0), (0, 1), (0, 2), (3, 2))[k]
        return copy(buf, role, j, 0, 2, y_s, y_r, k, y_dev)

    def x_send(buf, k):
        role, j = ((0, 0), (0, 1), (0, 2), (2, 1))[k]
        return copy(buf, role, j, 2, 2, x_s, x_r, k, x_dev)

    def x_recv(buf, k):
        role, j = ((1, 0), (1, 1), (1, 2), (3, 1))[k]
        return copy(buf, role, j, 2, 2, x_s, x_r, k, x_dev)

    def z_send(buf, k):
        role, j = ((0, 0), (0, 1), (0, 2), (1, 0))[k]
        return copy(buf, role, j, 2, 2, z_s, z_r, k, z_dev)

    def z_recv(buf, k):
        role, j = ((2, 0), (2, 1), (2, 2), (3, 0))[k]
        return copy(buf, role, j, 2, 2, z_s, z_r, k, z_dev)

    def n_copy(buf, role, j):
        return copy(buf, role, j, 2, 3, n_s, n_r, role * 3 + j, n_dev)

    def direct(buf):
        whole = (wqkv, wo)[buf]
        return pltpu.make_async_remote_copy(
            src_ref=whole.at[0], dst_ref=whole.at[1], send_sem=d_s.at[buf], recv_sem=d_r.at[buf],
            device_id=n_dev, device_id_type=MESH)

    def from_y(buf, k):
        y_wait = y_recv(buf, k)
        y_wait.wait_recv()
        if k < 3:
            go(x_send(buf, k))
            go(z_send(buf, k))
            go(n_copy(buf, 0, k))
        else:
            go(n_copy(buf, 3, 2))

    def y_recv(buf, k):
        return y_copy(buf, k)

    def from_x(buf, k):
        x_recv(buf, k).wait_recv()
        if k == 0:
            go(z_send(buf, 3))
        if k < 3:
            go(n_copy(buf, 1, k))
        else:
            go(n_copy(buf, 3, 1))

    def from_z(buf, k):
        z_recv(buf, k).wait_recv()
        if k == 1:
            go(x_send(buf, 3))
        if k < 3:
            go(n_copy(buf, 2, k))
        else:
            go(n_copy(buf, 3, 0))

    for c in load_w:
        c.wait()
    for k in range(4):
        go(y_copy(0, k))
    go(direct(0))
    load_h.wait()
    load_d.wait()
    load_o.wait()
    for k in range(4):
        go(y_copy(1, k))
    go(direct(1))

    def norm_rows(lo, hi):
        @pl.loop(lo // 16, hi // 16)
        def _(i):
            r = pl.ds(pl.multiple_of(i * 16, 16), 16)
            h = ext[r, :].astype(F32)
            ms = jnp.mean(h * h, axis=1, keepdims=True)
            normed[r, :] = (h * lax.rsqrt(ms + eps) * gain[...]).astype(BF).astype(F32)

    def conv_rows(lo, hi):
        @pl.loop(lo // 16, hi // 16)
        def _(i):
            block = normed[pl.ds(pl.multiple_of(i * 16 + PAD - 8, 8), 24), :]
            total = jnp.zeros((16, width), F32)
            for k in range(ntaps):
                total = total + taps[k : k + 1, :] * block[8 - k : 24 - k]
            mixed[pl.ds(pl.multiple_of(i * 16, 16), 16), :] = total.astype(BF)

    norm_rows(HALO, HALO + rows)
    conv_rows(WINDOW + 16, full)
    from_y(0, 0)

    @pl.when(has_prev)
    def _():
        halo_h.wait_recv()
        halo_d.wait_recv()

    @pl.when(jnp.logical_not(has_prev))
    def _():
        ext[0:HALO, :] = jnp.zeros((HALO, width), BF)
        docs[:, 0:WINDOW] = jnp.full((docs.shape[0], WINDOW), -1, jnp.int32)

    norm_rows(0, HALO)
    conv_rows(0, WINDOW + 16)

    blocks = rows // WINDOW
    span = 2 * WINDOW
    rel_r = lax.broadcasted_iota(jnp.int32, (WINDOW, span), 0)
    rel_c = lax.broadcasted_iota(jnp.int32, (WINDOW, span), 1)
    in_window = (rel_c > rel_r) & (rel_c <= rel_r + WINDOW)
    for i in range(blocks):
        qd = doc_col[i * WINDOW : (i + 1) * WINDOW, :]
        kd = docs[0:1, i * WINDOW : i * WINDOW + span]
        same = jnp.concatenate([qd, qd], axis=1) == kd
        bias[i] = jnp.where(in_window & same, 0.0, -jnp.inf)

    def turn(x, c, s):
        lane = lax.broadcasted_iota(jnp.int32, x.shape, 1)
        swapped = jnp.where(lane % HEAD < HEAD // 2, pltpu.roll(x, LANES - HEAD // 2, 1), pltpu.roll(x, HEAD // 2, 1))
        return x * c + swapped * s

    scale = 1.0 / math.sqrt(HEAD)

    def project(slot):
        @pl.loop(0, qc // 256)
        def _(n):
            c0 = pl.multiple_of(n * 256, 256)
            r = jnp.dot(mixed[WINDOW:, :], wqkv[slot, :, pl.ds(c0, 256)], preferred_element_type=F32)
            for h in range(2):
                piece = r[:, h * LANES : (h + 1) * LANES]
                q_s[n * 2 + h] = (turn(piece, cos[WINDOW:, :], sin[WINDOW:, :]) * scale).astype(BF)

        r = jnp.dot(mixed[...], wqkv[slot, :, qc:], preferred_element_type=F32)
        k = turn(r[:, :kc], cos[...], sin[...])
        v = r[:, kc:]
        low = lax.broadcasted_iota(jnp.int32, k.shape, 1) < HEAD
        kr, vr = pltpu.roll(k, HEAD, 1), pltpu.roll(v, HEAD, 1)
        k_s[0] = jnp.where(low, k, kr).astype(BF)
        k_s[1] = jnp.where(low, kr, k).astype(BF)
        ones = jnp.ones((full, LANES), BF)
        v_s[0, :, :LANES] = jnp.where(low, v, vr).astype(BF)
        v_s[1, :, :LANES] = jnp.where(low, vr, v).astype(BF)
        v_s[0, :, LANES:] = ones
        v_s[1, :, LANES:] = ones

    def attend(slot):
        @pl.loop(0, blocks)
        def _(i):
            r0 = pl.multiple_of(i * WINDOW, WINDOW)
            low = lax.broadcasted_iota(jnp.int32, (WINDOW, LANES), 1) < HEAD
            zero = jnp.zeros((WINDOW, LANES), BF)
            for g in range(2):
                stack = []
                for h in range(2):
                    qv = q_s[g * 2 + h, pl.ds(r0, WINDOW), :]
                    stack += [jnp.where(low, qv, zero), jnp.where(low, zero, qv)]
                qs = jnp.concatenate(stack, axis=0)
                ks = k_s[g, pl.ds(r0, span), :]
                s = lax.dot_general(qs, ks, (((1,), (1,)), ((), ())), preferred_element_type=F32)
                s = s.reshape(4, WINDOW, span) + bias[i][None]
                m = jnp.max(s, axis=2, keepdims=True)
                p = jnp.exp(s - m).astype(BF).reshape(4 * WINDOW, span)
                o = jnp.dot(p, v_s[g, pl.ds(r0, span), :], preferred_element_type=F32)
                o = o[:, :LANES] / o[:, LANES:]
                for h in range(2):
                    a = o[(2 * h) * WINDOW : (2 * h + 1) * WINDOW]
                    b = o[(2 * h + 1) * WINDOW : (2 * h + 2) * WINDOW]
                    c0 = (g * 2 + h) * LANES
                    att[slot % 2, pl.ds(r0, WINDOW), c0 : c0 + LANES] = jnp.where(low, a, b).astype(BF)

    def out_cols(first, c, n, last):
        two = None
        for s in range(2):
            r = jnp.dot(att[s], wo[first + s, :, pl.ds(c, n)], preferred_element_type=F32)
            two = r if two is None else two + r
        if last:
            two = two + acc[:, pl.ds(c, n)]
            out[:, pl.ds(c, n)] = (ext[HALO:, pl.ds(c, n)].astype(F32) + two).astype(BF)
        else:
            acc[:, pl.ds(c, n)] = two

    def project_out(first, last, lo, hi):
        @pl.loop(lo, hi)
        def _(n):
            out_cols(first, pl.multiple_of(n * 256, 256), 256, last)

    whole = width // 256
    rest = width - whole * 256

    project(0)
    from_y(0, 1)
    attend(0)
    from_x(0, 0)
    from_z(0, 0)
    direct(0).wait_recv()
    project(1)
    from_y(0, 2)
    from_x(0, 1)
    from_z(0, 1)
    attend(1)
    direct(1).wait_recv()
    project_out(0, False, 0, whole // 2)
    from_y(0, 3)
    from_x(0, 2)
    from_z(0, 2)
    project_out(0, False, whole // 2, whole)
    if rest:
        out_cols(0, whole * 256, rest, False)
    from_x(0, 3)
    from_z(0, 3)
    from_y(1, 0)
    project(2)
    from_y(1, 1)
    from_x(1, 0)
    from_z(1, 0)
    attend(2)
    for role in range(4):
        for j in range(3):
            n_copy(0, role, j).wait_recv()
    from_y(1, 2)
    from_x(1, 1)
    from_z(1, 1)
    project(3)
    from_y(1, 3)
    from_x(1, 2)
    from_z(1, 2)
    attend(3)
    from_x(1, 3)
    from_z(1, 3)
    for role in range(4):
        for j in range(3):
            n_copy(1, role, j).wait_recv()
    project_out(2, True, 0, whole)
    if rest:
        out_cols(2, whole * 256, rest, True)
    for c in sent:
        c.wait_send()

    @pl.when(has_next)
    def _():
        halo_h.wait_send()
        halo_d.wait_send()


def solution(mesh):
    seq_size, tensor_size = mesh.shape["seq"], mesh.shape["tensor"]

    def local(hidden_in, norm_gain, conv_weight, w_query, w_key, w_value, w_out, doc_ids):
        rows, width = hidden_in.shape
        qc, kc = w_query.shape[1], w_key.shape[1]
        full = rows + WINDOW
        tensor = lax.axis_index("tensor")
        begin = (lax.axis_index("seq") * tensor_size + tensor) * rows
        mine = lax.dynamic_slice_in_dim(doc_ids, tensor * rows, rows, 0)
        doc_row = jnp.broadcast_to(mine[None, :], (8, rows))
        doc_col = jnp.broadcast_to(mine[:, None], (rows, LANES))
        half = HEAD // 2
        frequency = jnp.exp(jnp.arange(half, dtype=F32) * (-2.0 * math.log(rope_base) / HEAD))
        positions = (begin - WINDOW + jnp.arange(full, dtype=jnp.int32)).astype(F32)
        angle = positions[:, None] * frequency[None, :]
        c, s = jnp.cos(angle), jnp.sin(angle)
        cos = jnp.concatenate([c, c, c, c], axis=1)
        sin = jnp.concatenate([-s, s, -s, s], axis=1)
        dma = pltpu.SemaphoreType.DMA
        vm, hb = pl.BlockSpec(memory_space=pltpu.VMEM), pl.BlockSpec(memory_space=pl.ANY)
        return pl.pallas_call(
            lambda *refs: kernel(seq_size, tensor_size, *refs),
            out_shape=jax.ShapeDtypeStruct((rows, width), BF),
            in_specs=[hb, vm, vm, hb, hb, hb, hb, hb, vm, vm, vm],
            out_specs=vm,
            scratch_shapes=[
                pltpu.VMEM((HALO + rows, width), BF),
                pltpu.VMEM((HALO + rows, width), F32),
                pltpu.VMEM((full, width), BF),
                pltpu.VMEM((4, width, qc + 2 * kc), BF),
                pltpu.VMEM((4, qc, width), BF),
                pltpu.VMEM((qc // LANES, rows, LANES), BF),
                pltpu.VMEM((2, full, LANES), BF),
                pltpu.VMEM((2, full, 2 * LANES), BF),
                pltpu.VMEM((2, rows, qc), BF),
                pltpu.VMEM((rows, width), F32),
                pltpu.VMEM((8, full), jnp.int32),
                pltpu.VMEM((rows // WINDOW, WINDOW, 2 * WINDOW), F32),
                dma((6,)),
                dma((2, 4)), dma((2, 4)),
                dma((2, 4)), dma((2, 4)),
                dma((2, 4)), dma((2, 4)),
                dma((2, 12)), dma((2, 12)),
                dma((2,)), dma((2,)),
                dma((2,)), dma((2,)),
            ],
            compiler_params=pltpu.CompilerParams(
                collective_id=0, has_side_effects=True, vmem_limit_bytes=67043328),
            name="block",
        )(hidden_in, norm_gain[None, :], conv_weight, w_query, w_key, w_value, w_out, doc_row, doc_col, cos, sin)

    in_specs = (
        P(("dp", "seq", "tensor"), None),
        P(),
        P(),
        P(None, "tensor"),
        P(None, "tensor"),
        P(None, "tensor"),
        P("tensor", None),
        P(("dp", "seq")),
    )
    out_specs = P(("dp", "seq", "tensor"), None)
    return jax.shard_map(local, mesh=mesh, in_specs=in_specs, out_specs=out_specs, check_vma=False)
```

time: 235 us -> 114 us (0.49)
  waiting for transfers between devices: 107 us -> 0 us
  Pallas kernels: 0 us -> 95.3 us
  matrix products: 52.4 us -> 0 us
  other arithmetic: 31.9 us -> 2.69 us
  between operations: 13.7 us -> 0.02 us
  starting transfers between devices: 12.6 us -> 0 us
  local copies, waits for them, and re-layouts: 12.9 us -> 15.8 us
  loops' own time: 2.61 us -> 0 us
    pallas_call x0 -> x1, Pallas kernels: none -> 95.3 us  [local(): pl.pallas_call(lambda *refs: kernel(seq_size, tensor_size, *refs), out_sh...]
    all_gather x2 -> x0, waiting for transfers between devices: 87.8 us -> none  [the longest x1 75.3 us: local(): piece = lax.all_gather(mixed, 'tensor', axis=0, tiled=True)]
    dot_general x12 -> x0, matrix products: 52.4 us -> none  [the longest x4 14.9 us: attend(): jnp.einsum('hgqk,khd->qhgd', rounded, values, preferred_element_type=jnp....]
    all_to_all x1 -> x0, waiting for transfers between devices: 16.5 us -> none  [local(): lax.all_to_all(attended, 'tensor', split_axis=0, concat_axis=1, tiled=True)]
    convert_element_type x4 -> x1, other arithmetic: 14.5 us -> 0.01 us  [local(): positions = (begin - WINDOW + jnp.arange(full, dtype=jnp.int32)).astype(F32)]
    reduce_sum x5 -> x0, other arithmetic: 11.4 us -> none  [the longest x4 8.69 us: attend(): total = jnp.sum(weights, axis=3)]
    ppermute x4 -> x0, starting transfers between devices: 7.88 us -> none  [passed_along(): return lax.ppermute(array, axis, pairs)]
    unnamed x14 -> x4, local copies, waits for them, and re-layouts: 1.62 us -> 7.61 us
  transfers between devices with their start and end apart: 7 -> 0, of which waited for: 5 -> 0; matrix products, arithmetic and copies ran while one was open for 26% -> 0% of each run, Pallas kernels for 0% -> 0%
where the time goes in v1:
time: 114 us
  Pallas kernels  95.3 us (84%)
  local copies, waits for them, and re-layouts  15.8 us (14%)
  other arithmetic  2.69 us (2%)
    pallas_call x1, Pallas kernels, local(): pl.pallas_call(lambda *refs: kernel(seq_size, tensor_size, *refs), out_sh...  95.3 us
    unnamed x4, local copies, waits for them, and re-layouts  7.61 us
    pallas_call x1, local copies, waits for them, and re-layouts, local(): pl.pallas_call(lambda *refs: kernel(seq_size, tensor_size, *refs), out_sh...  4.57 us

profile of v1, /device:TPU:27, one launch (start us, length us, event | category | flops | bytes accessed | tf_op | source)
XLA Modules:
  0.0 113.8 jit_solution(12167456544260919639)
XLA Ops:
  0.0 0.0 copy-start
  0.0 0.9 dynamic_slice.3
  0.9 1.3 %broadcast_in_dim.6.refs_1_ = f32[1,2880]{1,0:T(1,128)} reshape(f32[2880]{0:T(1024)} %param.9) | data formatting | bytes 23040 | tf_op jit(solution)/shard_map/broadcast_in_dim | solution.py:403
  2.2 0.6 broadcast_in_dim.7.refs_7_
  2.8 0.8 broadcast_in_dim.8.refs_8_
  3.7 1.2 %fusion = (f32[640,32]{1,0:T(8,128)S(1)}, f32[640,32]{1,0:T(8,128)S(1)}, f32[640,32]{1,0:T(8,128)S(1)}) fusion(f32[32]{0:T(128)S(1)} %multiply_exponential_fusion, f32[640]{0:T(1024)S(1)} %add_convert_fusion), kind=kLoop, calls=%fused_computation.4 | loop fusion | flops 40960 | bytes 248448 | tf_op jit(solution)/shard_map/neg | solution.py:371
  4.9 1.5 %pad_maximum_fusion = (f32[640,128]{1,0:T(8,128)}, f32[640,128]{1,0:T(8,128)}) fusion(f32[640,32]{1,0:T(8,128)S(1)} %get-tuple-element.7, f32[640,32]{1,0:T(8,128)S(1)} %get-tuple-element.6, f32[640,32]{1,0:T(8,128)S(1)} %get-tuple-element.5), kind=kLoop, calls=%fused_computation.2 | loop fusion | flops 491520 | bytes 901120 | tf_op jit(solution)/shard_map/concatenate | solution.py:370
  6.4 0.0 copy-done
  6.4 3.0 %copy.13.refs_0_ = bf16[512,2880]{1,0:T(8,128)(2,1)} copy(bf16[512,2880]{0,1:T(8,128)(2,1)S(1)} %copy-done) | data formatting | bytes 5898240 | tf_op args[0]
  9.4 4.6 %copy.14.refs_6_ = bf16[512,2880]{1,0:T(8,128)(2,1)} copy(bf16[512,2880]{0,1:T(8,128)(2,1)} %param.14) | data formatting | bytes 5898240 | tf_op args[6]
  14.0 95.3 %block.1 = bf16[512,2880]{1,0:T(8,128)(2,1)} custom-call(bf16[512,2880]{1,0:T(8,128)(2,1)} %copy.13.refs_0_, f32[1,2880]{1,0:T(1,128)} %broadcast_in_dim.6.refs_1_, f32[4,2880]{1,0:T(4,128)} %refs_2_.1, bf16[2880,512]{1,0:T(8,128)(2,1)} %refs_3_.1, bf16[2880,128]{1,0:T(8,128)(2,1)} %refs_4_.1, bf16[2880,128]{1,0:T(8,128)(2,1)} %refs_5_.1, ...), custom_call_target="tpu_custom_call" | custom-call | tf_op jit(solution)/shard_map/block/pallas_call | solution.py:374
  109.3 4.6 %copy.15 = bf16[512,2880]{0,1:T(8,128)(2,1)} copy(bf16[512,2880]{1,0:T(8,128)(2,1)} %block.1) | data formatting | bytes 5898240 | tf_op jit(solution)/shard_map/block/pallas_call | solution.py:374
  (2 shorter events, 0.0 us)
Async XLA Ops:
  0.0 6.4 %copy-start = (bf16[512,2880]{0,1:T(8,128)(2,1)S(1)}, bf16[512,2880]{0,1:T(8,128)(2,1)}, u32[]{:S(2)}) copy-start(bf16[512,2880]{0,1:T(8,128)(2,1)} %param.8) | copy-start | bytes 8847364

commit v2 on v1

--- a/solution.py
+++ b/solution.py
@@ -18,10 +18,10 @@
 F32 = jnp.float32
 
 
-def kernel(seq_size, tensor_size, hidden, gain, taps, wq, wk, wv, wout, doc_row, doc_col, cos, sin, out,
-           ext, normed, mixed, wqkv, wo, q_s, k_s, v_s, att, acc, docs, bias,
+def kernel(seq_size, tensor_size, hidden, gain, taps, wq, wk, wv, wout, halo, doc_row, cos, sin, out,
+           own, ext, normed, mixed, wqkv, wo, q_s, k_s, v_s, att, acc, docs, bias,
            load_sem, y_s, y_r, x_s, x_r, z_s, z_r, n_s, n_r, d_s, d_r, h_s, h_r):
-    rows, width = hidden.shape
+    width, rows = hidden.shape
     qc, kc = wq.shape[1], wk.shape[1]
     cols = qc + 2 * kc
     ntaps = taps.shape[0]
@@ -61,7 +61,7 @@
         pltpu.make_async_copy(wv, wqkv.at[0, :, pl.ds(qc + kc, kc)], load_sem.at[2]),
     ]
     load_o = pltpu.make_async_copy(wout, wo.at[0], load_sem.at[3])
-    load_h = pltpu.make_async_copy(hidden, ext.at[pl.ds(HALO, rows)], load_sem.at[4])
+    load_h = pltpu.make_async_copy(hidden, own, load_sem.at[4])
     load_d = pltpu.make_async_copy(doc_row, docs.at[:, pl.ds(WINDOW, rows)], load_sem.at[5])
     for c in load_w:
         c.start()
@@ -71,7 +71,7 @@
     pl.semaphore_wait(barrier, 4 + jnp.where(has_prev, 1, 0) + jnp.where(has_next, 1, 0))
 
     halo_h = pltpu.make_async_remote_copy(
-        src_ref=hidden.at[pl.ds(rows - HALO, HALO)], dst_ref=ext.at[pl.ds(0, HALO)],
+        src_ref=halo, dst_ref=ext.at[pl.ds(0, HALO)],
         send_sem=h_s.at[0], recv_sem=h_r.at[0], device_id=next_dev, device_id_type=MESH)
     halo_d = pltpu.make_async_remote_copy(
         src_ref=doc_row.at[:, pl.ds(rows - WINDOW, WINDOW)], dst_ref=docs.at[:, pl.ds(0, WINDOW)],
@@ -82,15 +82,11 @@
         halo_h.start()
         halo_d.start()
 
-    wrow, orow = width // 4, qc // 4
+    wrow = width // 4
     wpart = wrow // 3
-    osize = (48, 48, 32) if orow == 128 else (orow // 2, orow // 4, orow // 4)
-    ostart = (0, osize[0], osize[0] + osize[1])
 
     def part(buf, slot, q, j):
-        if buf == 0:
-            return wqkv.at[slot, pl.ds(pl.multiple_of(q * wrow + j * wpart, 16), wpart)]
-        return wo.at[slot, pl.ds(pl.multiple_of(q * orow + ostart[j], 16), osize[j])]
+        return (wqkv, wo)[buf].at[slot, pl.ds(pl.multiple_of(q * wrow + j * wpart, 16), wpart)]
 
     xb, zb = seq % 2, dp % 2
     quarter = (xb * 2 + zb, (1 - xb) * 2 + zb, xb * 2 + 1 - zb, (1 - xb) * 2 + 1 - zb)
@@ -194,6 +190,15 @@
                 total = total + taps[k : k + 1, :] * block[8 - k : 24 - k]
             mixed[pl.ds(pl.multiple_of(i * 16, 16), 16), :] = total.astype(BF)
 
+    def flip(c, n):
+        ext[HALO:, pl.ds(c, n)] = own[pl.ds(c, n), :].astype(F32).T.astype(BF)
+
+    @pl.loop(0, width // LANES)
+    def _(i):
+        flip(pl.multiple_of(i * LANES, LANES), LANES)
+
+    if width % LANES:
+        flip(width // LANES * LANES, width % LANES)
     norm_rows(HALO, HALO + rows)
     conv_rows(WINDOW + 16, full)
     from_y(0, 0)
@@ -217,8 +222,9 @@
     rel_c = lax.broadcasted_iota(jnp.int32, (WINDOW, span), 1)
     in_window = (rel_c > rel_r) & (rel_c <= rel_r + WINDOW)
     for i in range(blocks):
-        qd = doc_col[i * WINDOW : (i + 1) * WINDOW, :]
-        kd = docs[0:1, i * WINDOW : i * WINDOW + span]
+        qd = docs[0:1, (i + 1) * WINDOW : (i + 2) * WINDOW].astype(F32)
+        qd = jnp.broadcast_to(qd, (WINDOW, WINDOW)).T
+        kd = docs[0:1, i * WINDOW : i * WINDOW + span].astype(F32)
         same = jnp.concatenate([qd, qd], axis=1) == kd
         bias[i] = jnp.where(in_window & same, 0.0, -jnp.inf)
 
@@ -274,26 +280,20 @@
                     a = o[(2 * h) * WINDOW : (2 * h + 1) * WINDOW]
                     b = o[(2 * h + 1) * WINDOW : (2 * h + 2) * WINDOW]
                     c0 = (g * 2 + h) * LANES
-                    att[slot % 2, pl.ds(r0, WINDOW), c0 : c0 + LANES] = jnp.where(low, a, b).astype(BF)
-
-    def out_cols(first, c, n, last):
-        two = None
-        for s in range(2):
-            r = jnp.dot(att[s], wo[first + s, :, pl.ds(c, n)], preferred_element_type=F32)
-            two = r if two is None else two + r
-        if last:
-            two = two + acc[:, pl.ds(c, n)]
-            out[:, pl.ds(c, n)] = (ext[HALO:, pl.ds(c, n)].astype(F32) + two).astype(BF)
-        else:
-            acc[:, pl.ds(c, n)] = two
+                    att[slot % 2, c0 : c0 + LANES, pl.ds(r0, WINDOW)] = jnp.where(low, a, b).T.astype(BF)
+
+    step = width // 6
 
     def project_out(first, last, lo, hi):
         @pl.loop(lo, hi)
         def _(n):
-            out_cols(first, pl.multiple_of(n * 256, 256), 256, last)
-
-    whole = width // 256
-    rest = width - whole * 256
+            r = pl.ds(pl.multiple_of(n * step, 16), step)
+            two = jnp.dot(wo[first, r, :], att[0], preferred_element_type=F32)
+            two = two + jnp.dot(wo[first + 1, r, :], att[1], preferred_element_type=F32)
+            if last:
+                out[r, :] = (own[r, :].astype(F32) + (two + acc[r, :])).astype(BF)
+            else:
+                acc[r, :] = two
 
     project(0)
     from_y(0, 1)
@@ -307,13 +307,11 @@
     from_z(0, 1)
     attend(1)
     direct(1).wait_recv()
-    project_out(0, False, 0, whole // 2)
+    project_out(0, False, 0, 3)
     from_y(0, 3)
     from_x(0, 2)
     from_z(0, 2)
-    project_out(0, False, whole // 2, whole)
-    if rest:
-        out_cols(0, whole * 256, rest, False)
+    project_out(0, False, 3, 6)
     from_x(0, 3)
     from_z(0, 3)
     from_y(1, 0)
@@ -338,9 +336,7 @@
     for role in range(4):
         for j in range(3):
             n_copy(1, role, j).wait_recv()
-    project_out(2, True, 0, whole)
-    if rest:
-        out_cols(2, whole * 256, rest, True)
+    project_out(2, True, 0, 6)
     for c in sent:
         c.wait_send()
 
@@ -361,32 +357,32 @@
         begin = (lax.axis_index("seq") * tensor_size + tensor) * rows
         mine = lax.dynamic_slice_in_dim(doc_ids, tensor * rows, rows, 0)
         doc_row = jnp.broadcast_to(mine[None, :], (8, rows))
-        doc_col = jnp.broadcast_to(mine[:, None], (rows, LANES))
         half = HEAD // 2
-        frequency = jnp.exp(jnp.arange(half, dtype=F32) * (-2.0 * math.log(rope_base) / HEAD))
+        lane = jnp.arange(LANES, dtype=jnp.int32)
+        frequency = jnp.exp((lane % half).astype(F32) * (-2.0 * math.log(rope_base) / HEAD))
         positions = (begin - WINDOW + jnp.arange(full, dtype=jnp.int32)).astype(F32)
         angle = positions[:, None] * frequency[None, :]
-        c, s = jnp.cos(angle), jnp.sin(angle)
-        cos = jnp.concatenate([c, c, c, c], axis=1)
-        sin = jnp.concatenate([-s, s, -s, s], axis=1)
+        cos = jnp.cos(angle)
+        sin = jnp.sin(angle) * jnp.where(lane % HEAD < half, -1.0, 1.0)[None, :]
         dma = pltpu.SemaphoreType.DMA
         vm, hb = pl.BlockSpec(memory_space=pltpu.VMEM), pl.BlockSpec(memory_space=pl.ANY)
         return pl.pallas_call(
             lambda *refs: kernel(seq_size, tensor_size, *refs),
-            out_shape=jax.ShapeDtypeStruct((rows, width), BF),
-            in_specs=[hb, vm, vm, hb, hb, hb, hb, hb, vm, vm, vm],
+            out_shape=jax.ShapeDtypeStruct((width, rows), BF),
+            in_specs=[hb, vm, vm, hb, hb, hb, hb, hb, hb, vm, vm],
             out_specs=vm,
             scratch_shapes=[
+                pltpu.VMEM((width, rows), BF),
                 pltpu.VMEM((HALO + rows, width), BF),
                 pltpu.VMEM((HALO + rows, width), F32),
                 pltpu.VMEM((full, width), BF),
                 pltpu.VMEM((4, width, qc + 2 * kc), BF),
-                pltpu.VMEM((4, qc, width), BF),
+                pltpu.VMEM((4, width, qc), BF),
                 pltpu.VMEM((qc // LANES, rows, LANES), BF),
                 pltpu.VMEM((2, full, LANES), BF),
                 pltpu.VMEM((2, full, 2 * LANES), BF),
-                pltpu.VMEM((2, rows, qc), BF),
-                pltpu.VMEM((rows, width), F32),
+                pltpu.VMEM((2, qc, rows), BF),
+                pltpu.VMEM((width, rows), F32),
                 pltpu.VMEM((8, full), jnp.int32),
                 pltpu.VMEM((rows // WINDOW, WINDOW, 2 * WINDOW), F32),
                 dma((6,)),
@@ -400,7 +396,8 @@
             compiler_params=pltpu.CompilerParams(
                 collective_id=0, has_side_effects=True, vmem_limit_bytes=67043328),
             name="block",
-        )(hidden_in, norm_gain[None, :], conv_weight, w_query, w_key, w_value, w_out, doc_row, doc_col, cos, sin)
+        )(hidden_in.T, norm_gain[None, :], conv_weight, w_query, w_key, w_value, w_out.T,
+          hidden_in[rows - HALO :], doc_row, cos, sin).T
 
     in_specs = (
         P(("dp", "seq", "tensor"), None),

time: 114 us -> 104 us (0.912)
  local copies, waits for them, and re-layouts: 15.8 us -> 9.9 us
  Pallas kernels: 95.3 us -> 91.8 us
    pallas_call x1 -> x0, local copies, waits for them, and re-layouts: 4.57 us -> none  [local(): pl.pallas_call(lambda *refs: kernel(seq_size, tensor_size, *refs), out_sh...]
    pallas_call x1, Pallas kernels: 95.3 us -> 91.8 us  [local(): pl.pallas_call(lambda *refs: kernel(seq_size, tensor_size, *refs), out_sh...]
    unnamed x4 -> x2, local copies, waits for them, and re-layouts: 7.61 us -> 5.21 us
    mul x0 -> x1, other arithmetic: none -> 2.07 us  [local(): sin = jnp.sin(angle) * jnp.where(lane % HEAD < half, -1.0, 1.0)[None, :]]
    slice x0 -> x1, local copies, waits for them, and re-layouts: none -> 2.01 us  [local(): hidden_in[rows - HALO:]]
    concatenate x1 -> x0, other arithmetic: 1.46 us -> none  [local(): cos = jnp.concatenate([c, c, c, c], axis=1)]
    neg x1 -> x0, other arithmetic: 1.21 us -> none  [local(): sin = jnp.concatenate([-s, s, -s, s], axis=1)]
where the time goes in v2:
time: 104 us
  Pallas kernels  91.8 us (88%)
  local copies, waits for them, and re-layouts  9.9 us (10%)
  other arithmetic  2.08 us (2%)
    pallas_call x1, Pallas kernels, local(): pl.pallas_call(lambda *refs: kernel(seq_size, tensor_size, *refs), out_sh...  91.8 us
    unnamed x2, local copies, waits for them, and re-layouts  5.21 us

profile of v2, /device:TPU:27, one launch (start us, length us, event | category | flops | bytes accessed | tf_op | source)
XLA Modules:
  0.0 103.8 jit_solution(14356718203608177106)
XLA Ops:
  0.0 0.8 dynamic_slice.3
  0.8 1.3 %broadcast_in_dim.20.refs_1_ = f32[1,2880]{1,0:T(1,128)} reshape(f32[2880]{0:T(1024)} %param.9) | data formatting | bytes 23040 | tf_op jit(solution)/shard_map/broadcast_in_dim | solution.py:399
  2.1 0.6 broadcast_in_dim.21.refs_8_
  2.7 2.1 %fusion = (f32[640,128]{1,0:T(8,128)}, f32[640,128]{1,0:T(8,128)}) fusion(f32[128]{0:T(128)S(1)} %get-tuple-element.7, f32[128]{0:T(128)S(1)} %get-tuple-element.8, f32[640]{0:T(1024)S(1)} %add_convert_fusion), kind=kLoop, calls=%fused_computation.2 | loop fusion | flops 163840 | bytes 658944 | tf_op jit(solution)/shard_map/mul | solution.py:366
  4.8 2.0 %slice.3 = bf16[144,2880]{0,1:T(8,128)(2,1)S(1)} slice(bf16[512,2880]{0,1:T(8,128)(2,1)} %param.8), slice={[368:512], [0:2880]} | slice | bytes 1658880 | tf_op jit(solution)/shard_map/slice | solution.py:400
  6.8 1.6 %copy.10.refs_7_ = bf16[144,2880]{1,0:T(8,128)(2,1)} copy(bf16[144,2880]{0,1:T(8,128)(2,1)S(1)} %slice.3) | data formatting | bytes 1658880
  8.4 91.8 %block.1 = bf16[2880,512]{1,0:T(8,128)(2,1)} custom-call(bf16[2880,512]{1,0:T(8,128)(2,1)} %bitcast.4, f32[1,2880]{1,0:T(1,128)} %broadcast_in_dim.20.refs_1_, f32[4,2880]{1,0:T(4,128)} %refs_2_.1, bf16[2880,512]{1,0:T(8,128)(2,1)} %refs_3_.1, bf16[2880,128]{1,0:T(8,128)(2,1)} %refs_4_.1, bf16[2880,128]{1,0:T(8,128)(2,1)} %refs_5_.1, ...), custom_call_target="tpu_custom_call" | custom-call | tf_op jit(solution)/shard_map/block/pallas_call | solution.py:369
  100.2 3.6 %copy.12 = bf16[512,2880]{0,1:T(8,128)(2,1)} copy(bf16[512,2880]{0,1:T(8,128)(2,1)} %bitcast.3) | data formatting | bytes 5898240
  (2 shorter events, 0.0 us)

commit v3 on v2

--- a/solution.py
+++ b/solution.py
@@ -77,11 +77,6 @@
         src_ref=doc_row.at[:, pl.ds(rows - WINDOW, WINDOW)], dst_ref=docs.at[:, pl.ds(0, WINDOW)],
         send_sem=h_s.at[1], recv_sem=h_r.at[1], device_id=next_dev, device_id_type=MESH)
 
-    @pl.when(has_next)
-    def _():
-        halo_h.start()
-        halo_d.start()
-
     wrow = width // 4
     wpart = wrow // 3
 
@@ -163,7 +158,14 @@
 
     for c in load_w:
         c.wait()
-    for k in range(4):
+    go(y_copy(0, 0))
+
+    @pl.when(has_next)
+    def _():
+        halo_h.start()
+        halo_d.start()
+
+    for k in range(1, 4):
         go(y_copy(0, k))
     go(direct(0))
     load_h.wait()

time: 104 us -> 111 us (1.067)
  the two profiles are of different devices: /device:TPU:27 before, /device:TPU:7 now
where the time goes in v3:
time: 111 us; the launch traced here: 110 us
  Pallas kernels  98.4 us (89%)
  local copies, waits for them, and re-layouts  9.9 us (9%)
  other arithmetic  2.08 us (2%)
    pallas_call x1, Pallas kernels, local(): pl.pallas_call(lambda *refs: kernel(seq_size, tensor_size, *refs), out_sh...  98.4 us
    unnamed x2, local copies, waits for them, and re-layouts  5.21 us

profile of v3, /device:TPU:7, one launch (start us, length us, event | category | flops | bytes accessed | tf_op | source)
XLA Modules:
  0.0 110.4 jit_solution(7219325662785271887)
XLA Ops:
  0.0 0.8 dynamic_slice.3
  0.8 1.3 %broadcast_in_dim.20.refs_1_ = f32[1,2880]{1,0:T(1,128)} reshape(f32[2880]{0:T(1024)} %param.9) | data formatting | bytes 23040 | tf_op jit(solution)/shard_map/broadcast_in_dim | solution.py:401
  2.1 0.6 broadcast_in_dim.21.refs_8_
  2.7 2.1 %fusion = (f32[640,128]{1,0:T(8,128)}, f32[640,128]{1,0:T(8,128)}) fusion(f32[128]{0:T(128)S(1)} %get-tuple-element.7, f32[128]{0:T(128)S(1)} %get-tuple-element.8, f32[640]{0:T(1024)S(1)} %add_convert_fusion), kind=kLoop, calls=%fused_computation.2 | loop fusion | flops 163840 | bytes 658944 | tf_op jit(solution)/shard_map/mul | solution.py:368
  4.8 2.0 %slice.3 = bf16[144,2880]{0,1:T(8,128)(2,1)S(1)} slice(bf16[512,2880]{0,1:T(8,128)(2,1)} %param.8), slice={[368:512], [0:2880]} | slice | bytes 1658880 | tf_op jit(solution)/shard_map/slice | solution.py:402
  6.8 1.6 %copy.10.refs_7_ = bf16[144,2880]{1,0:T(8,128)(2,1)} copy(bf16[144,2880]{0,1:T(8,128)(2,1)S(1)} %slice.3) | data formatting | bytes 1658880
  8.4 98.4 %block.1 = bf16[2880,512]{1,0:T(8,128)(2,1)} custom-call(bf16[2880,512]{1,0:T(8,128)(2,1)} %bitcast.4, f32[1,2880]{1,0:T(1,128)} %broadcast_in_dim.20.refs_1_, f32[4,2880]{1,0:T(4,128)} %refs_2_.1, bf16[2880,512]{1,0:T(8,128)(2,1)} %refs_3_.1, bf16[2880,128]{1,0:T(8,128)(2,1)} %refs_4_.1, bf16[2880,128]{1,0:T(8,128)(2,1)} %refs_5_.1, ...), custom_call_target="tpu_custom_call" | custom-call | tf_op jit(solution)/shard_map/block/pallas_call | solution.py:371
  106.8 3.6 %copy.12 = bf16[512,2880]{0,1:T(8,128)(2,1)} copy(bf16[512,2880]{0,1:T(8,128)(2,1)} %bitcast.3) | data formatting | bytes 5898240
  (2 shorter events, 0.0 us)
